TPU v7x, 32 devices: a whole 2x2x4 slice. The times are simulated.
32 devices in a mesh: dp: 2 (over x), expert: 16 (over z, y, core).
Axes of the slice: x: 2, y: 2, z: 4, core: 2. Of those that a mesh axis runs over, the one named last changes fastest.
Arguments:
- gradients: bfloat16 [16, 1024, 5888], P(None, ('dp', 'expert')), may hold values from -6 to 6
- momentum: bfloat16 [16, 1024, 5888], P('expert', 'dp'), may hold values from -6 to 6
- right_factor: bfloat16 [16, 5888, 256], P('expert', 'dp'), may hold values from -6 to 6
Outputs:
- new_momentum: bfloat16 [16, 1024, 5888], P('expert', 'dp')
- new_factor: bfloat16 [16, 5888, 256], P('expert', 'dp')
- update_rows: bfloat16 [16, 1024, 5888], P(None, ('dp', 'expert'))
All inputs are finite; a program needn't handle non-finite values.
Results may differ from a plain program's by a relative error of at most 0.009.
Values may be sent and summed in bfloat16 or wider, within the bound.
A program may use at most 128 MiB of HBM per device.

v0:
```python
import math

import jax
import jax.numpy as jnp
from jax import lax
from jax.experimental import pallas as pl
from jax.experimental.pallas import tpu as pltpu
from jax.sharding import PartitionSpec as P

decay_rate = 0.95
epsilon = 1e-06
CHUNKS = 2


def dot(a, b, contract=(1, 0)):
    return lax.dot_general(
        a,
        b,
        (((contract[0],), (contract[1],)), ((), ())),
        precision=lax.Precision.HIGHEST,
        preferred_element_type=jnp.float32,
    )


def inverted(lower):
    rank = lower.shape[0]
    row = lax.broadcasted_iota(jnp.int32, lower.shape, 0)
    col = lax.broadcasted_iota(jnp.int32, lower.shape, 1)
    diagonal = jnp.sum(jnp.where(row == col, lower, 0.0), axis=1, keepdims=True)
    result = jnp.where(row == col, 1.0 / diagonal, 0.0)
    size = 1
    while size < rank:
        inside = (row // (2 * size) == col // (2 * size)) & (row // size > col // size)
        below = jnp.where(inside, lower, 0.0)
        result = result - dot(result, dot(below, result))
        size *= 2
    return result


def panel_kernel(lower, gram, inverse, below, rest):
    half = lower.shape[0]
    inverse[...] = inverted(lower[...])
    below[...] = dot(gram[half:, :half], inverse[...], (1, 1))
    rest[...] = gram[half:, half:] - dot(below[...], below[...], (1, 1))


def join_kernel(lower, first, below, out):
    half = lower.shape[0]
    second = inverted(lower[...])
    out[:half, :half] = first[...]
    out[:half, half:] = jnp.zeros_like(second)
    out[half:, :half] = -dot(second, dot(below[...], first[...]))
    out[half:, half:] = second


def cholesky_inverse(gram):
    half = gram.shape[0] // 2
    block = jax.ShapeDtypeStruct((half, half), jnp.float32)
    vmem = pl.BlockSpec(memory_space=pltpu.VMEM)
    lower = lax.linalg.cholesky(gram[:half, :half], symmetrize_input=False)
    first, below, rest = pl.pallas_call(
        panel_kernel,
        out_shape=(block, block, block),
        in_specs=[vmem] * 2,
        out_specs=(vmem, vmem, vmem),
        name="cholesky_panel",
    )(lower, gram)
    lower = lax.linalg.cholesky(rest, symmetrize_input=False)
    return pl.pallas_call(
        join_kernel,
        out_shape=jax.ShapeDtypeStruct(gram.shape, jnp.float32),
        in_specs=[vmem] * 3,
        out_specs=vmem,
        name="cholesky_join",
    )(lower, first, below)


def make_body(dp):
    def others(value, wire=None):
        sent = value if wire is None else value.astype(wire)
        for step in range(1, dp):
            yield step, lax.ppermute(sent, "dp", [(i, (i + step) % dp) for i in range(dp)])

    def body(gradients, momentum, right_factor):
        place = lax.axis_index("dp")
        experts = gradients.shape[0]
        rows, width = momentum.shape[1], momentum.shape[2]
        depth, rank = right_factor.shape[1], right_factor.shape[2]
        factor = jnp.zeros((dp * depth, rank), right_factor.dtype)
        factor = lax.dynamic_update_slice(factor, right_factor[0], (place * depth, 0))
        for step, block in others(right_factor[0]):
            factor = lax.dynamic_update_slice(factor, block, ((place - step) % dp * depth, 0))
        arrived = lax.all_to_all(gradients, "expert", split_axis=0, concat_axis=0, tiled=True)
        arrived = arrived.reshape(rows, width)
        blended = (
            decay_rate * momentum[0].astype(jnp.float32) + arrived.astype(jnp.float32)
        ).astype(jnp.bfloat16)
        left = jnp.dot(blended, factor, preferred_element_type=jnp.float32)
        gram = jnp.dot(left.T, left, precision=lax.Precision.HIGHEST)
        gram_matrix = gram
        for _, block in others(gram):
            gram_matrix = gram_matrix + block
        inverse = cholesky_inverse(gram_matrix)
        ortho = jnp.dot(left, inverse.T, precision=lax.Precision.HIGHEST).astype(jnp.bfloat16)
        pieces = CHUNKS if width % (128 * CHUNKS) == 0 else 1
        size = width // pieces
        rights = []
        for k in range(pieces):
            part = lax.dot_general(
                blended[:, k * size : (k + 1) * size],
                ortho,
                (((0,), (0,)), ((), ())),
                preferred_element_type=jnp.float32,
            )
            total = part
            for _, block in others(part, jnp.bfloat16):
                total = total + block.astype(jnp.float32)
            rights.append(total)
        right = jnp.concatenate(rights, axis=0)
        column = jnp.sum(right * right, axis=0)
        new_factor = (right * lax.rsqrt(column / width + epsilon)).astype(jnp.bfloat16)
        update = (
            math.sqrt(rows * dp / rank)
            * lax.dot_general(
                ortho, new_factor, (((1,), (1,)), ((), ())), preferred_element_type=jnp.float32
            )
        ).astype(jnp.bfloat16)
        returned = lax.all_to_all(
            update.reshape(experts, rows // experts, width),
            "expert",
            split_axis=0,
            concat_axis=0,
            tiled=True,
        )
        kept = (
            blended.astype(jnp.float32)
            - (1.0 - decay_rate)
            * lax.dot_general(
                ortho,
                right.astype(jnp.bfloat16),
                (((1,), (1,)), ((), ())),
                preferred_element_type=jnp.float32,
            )
        ).astype(jnp.bfloat16)
        own_factor = lax.dynamic_slice(new_factor, (place * depth, 0), (depth, rank))
        return kept[None], own_factor[None], returned

    return body


def solution(mesh):
    in_specs = (P(None, ("dp", "expert"), None), P("expert", "dp", None), P("expert", "dp", None))
    out_specs = (P("expert", "dp", None), P("expert", "dp", None), P(None, ("dp", "expert"), None))
    return jax.shard_map(
        make_body(mesh.shape["dp"]),
        mesh=mesh,
        in_specs=in_specs,
        out_specs=out_specs,
        check_vma=False,
    )
```

profile of v0, /device:TPU:13, one launch (start us, length us, event | category | flops | bytes accessed | tf_op | source)
XLA Modules:
  0.0 420.4 jit_solution(15448430435274667587)
XLA Ops:
  0.6 0.0 copy-start.4
  0.6 6.7 %all-to-all-start = ((bf16[16,32,5888]{2,1,0:T(8,128)(2,1)}), bf16[16,32,5888]{2,1,0:T(8,128)(2,1)}, u32[]{:S(2)}, u32[]{:S(2)}) async-start(bf16[16,32,5888]{2,1,0:T(8,128)(2,1)} %param.4), calls=%async_computation | async-start | bytes 12058624 | tf_op jit(solution)/shard_map/all_to_all | solution.py:93
  7.3 0.0 copy-done.4
  7.3 1.3 collective-permute-start
  8.6 1.8 broadcast_in_dim.10
  10.4 1.2 constant_dynamic-update-slice_fusion.1
  11.6 30.0 %collective-permute-done = bf16[2944,256]{1,0:T(8,128)(2,1)S(1)} collective-permute-done((bf16[2944,256]{1,0:T(8,128)(2,1)S(1)}, bf16[2944,256]{1,0:T(8,128)(2,1)S(1)}, u32[]{:S(2)}, u32[]{:S(2)}) %collective-permute-start) | collective-permute-done | bytes 1507360 | tf_op jit(solution)/shard_map/ppermute | solution.py:82
  41.6 1.2 constant_dynamic-update-slice_fusion
  42.9 96.2 %all-to-all-done = bf16[16,32,5888]{2,1,0:T(8,128)(2,1)} async-done(((bf16[16,32,5888]{2,1,0:T(8,128)(2,1)}), bf16[16,32,5888]{2,1,0:T(8,128)(2,1)}, u32[]{:S(2)}, u32[]{:S(2)}) %all-to-all-start) | async-done | bytes 6029344 | tf_op jit(solution)/shard_map/all_to_all | solution.py:93
  139.1 6.2 %fusion = bf16[512,5888]{1,0:T(8,128)(2,1)S(1)} fusion(bf16[1,512,5888]{2,1,0:T(8,128)(2,1)} %param.5, bf16[16,32,5888]{2,1,0:T(8,128)(2,1)} %all-to-all-done), kind=kLoop, calls=%fused_computation.1 | loop fusion | flops 15073280 | bytes 18087936 | tf_op jit(solution)/shard_map/convert_element_type | solution.py:97
  145.3 0.0 copy-start
  145.4 5.8 %fusion.13 = f32[512,256]{1,0:T(8,128)S(1)} fusion(bf16[512,5888]{1,0:T(8,128)(2,1)S(1)} %fusion, bf16[5888,256]{1,0:T(8,128)(2,1)} %constant_dynamic-update-slice_fusion), kind=kOutput, calls=%fused_computation.32 | convolution fusion | flops 1543503872 | bytes 9568256 | tf_op jit(solution)/shard_map/dot_general | solution.py:98
  151.1 0.0 copy-done
  151.1 1.1 fusion.14
  152.2 1.3 collective-permute-start.1
  153.5 6.5 %collective-permute-done.1 = f32[256,256]{1,0:T(8,128)S(1)} collective-permute-done((f32[256,256]{1,0:T(8,128)S(1)}, f32[256,256]{1,0:T(8,128)S(1)}, u32[]{:S(2)}, u32[]{:S(2)}) %collective-permute-start.1) | collective-permute-done | bytes 262176 | tf_op jit(solution)/shard_map/ppermute | solution.py:82
  160.0 0.0 copy-start.5
  160.1 11.7 %custom-call.4 = f32[128,128]{1,0:T(8,128)S(1)} custom-call(f32[128,128]{1,0:T(8,128)S(1)} %slice.14), custom_call_target="Cholesky" | custom-call | tf_op jit(solution)/shard_map/cholesky/custom-call.1 | solution.py:60
  171.8 0.7 compare_reduce_fusion.1
  172.5 1.3 select_select_fusion.1.lower
  173.9 5.4 %cholesky_panel.1 = (f32[128,128]{1,0:T(8,128)}, f32[128,128]{1,0:T(8,128)}, f32[128,128]{1,0:T(8,128)}) custom-call(f32[128,128]{1,0:T(8,128)} %select_select_fusion.1.lower, f32[256,256]{1,0:T(8,128)} %copy-done.5), custom_call_target="tpu_custom_call" | custom-call | tf_op jit(solution)/shard_map/cholesky_panel/pallas_call | solution.py:61
  179.3 12.7 %custom-call.5 = f32[128,128]{1,0:T(8,128)S(1)} custom-call(f32[128,128]{1,0:T(8,128)} %get-tuple-element.7), custom_call_target="Cholesky" | custom-call | tf_op jit(solution)/shard_map/cholesky/custom-call.1 | solution.py:68
  192.0 0.6 compare_reduce_fusion
  192.6 1.3 select_select_fusion.lower
  193.9 5.0 %cholesky_join.1 = f32[256,256]{1,0:T(8,128)} custom-call(f32[128,128]{1,0:T(8,128)} %select_select_fusion.lower, f32[128,128]{1,0:T(8,128)} %get-tuple-element.8.first, f32[128,128]{1,0:T(8,128)} %get-tuple-element.9.below), custom_call_target="tpu_custom_call" | custom-call | tf_op jit(solution)/shard_map/cholesky_join/pallas_call | solution.py:69
  198.9 1.7 convolution_convert_fusion
  200.6 0.0 slice-start.1
  200.6 3.0 fusion.11
  203.6 1.3 collective-permute-start.3
  204.9 0.0 slice-done
  204.9 1.0 fusion.12
  205.9 0.3 collective-permute-start.2
  206.2 31.0 %collective-permute-done.3 = bf16[2944,256]{1,0:T(8,128)(2,1)S(1)} collective-permute-done((bf16[2944,256]{1,0:T(8,128)(2,1)S(1)}, bf16[2944,256]{1,0:T(8,128)(2,1)S(1)}, u32[]{:S(2)}, u32[]{:S(2)}) %collective-permute-start.3) | collective-permute-done | bytes 1507360 | tf_op jit(solution)/shard_map/ppermute | solution.py:82
  237.3 0.3 convert_add_fusion.1
  237.6 32.0 %collective-permute-done.2 = bf16[2944,256]{1,0:T(8,128)(2,1)S(1)} collective-permute-done((bf16[2944,256]{1,0:T(8,128)(2,1)S(1)}, bf16[2944,256]{1,0:T(8,128)(2,1)S(1)}, u32[]{:S(2)}, u32[]{:S(2)}) %collective-permute-start.2) | collective-permute-done | bytes 1507360 | tf_op jit(solution)/shard_map/ppermute | solution.py:82
  269.6 0.3 convert_add_fusion.2
  269.9 0.0 copy-start.1
  269.9 0.8 multiply_reduce_fusion
  270.7 0.8 copy-done.1
  271.5 0.5 multiply_convert_fusion.1
  272.0 0.0 copy-start.3
  272.0 4.4 %multiply_convert_fusion = bf16[512,5888]{1,0:T(8,128)(2,1)} fusion(bf16[512,256]{1,0:T(8,128)(2,1)S(1)} %convolution_convert_fusion, bf16[5888,256]{1,0:T(8,128)(2,1)S(1)} %multiply_convert_fusion.1), kind=kOutput, calls=%fused_computation.2 | convolution fusion | flops 1549533184 | bytes 9306112 | tf_op jit(solution)/shard_map/dot_general | solution.py:124
  276.4 6.5 %all-to-all-start.1 = ((bf16[16,32,5888]{2,1,0:T(8,128)(2,1)}), bf16[16,32,5888]{2,1,0:T(8,128)(2,1)}, u32[]{:S(2)}, u32[]{:S(2)}) async-start(bf16[16,32,5888]{2,1,0:T(8,128)(2,1)} %bitcast.25), calls=%async_computation.1 | async-start | bytes 12058624 | tf_op jit(solution)/shard_map/all_to_all | solution.py:128
  282.9 2.8 dynamic-slice_bitcast_fusion
  285.6 0.0 copy-done.2
  285.6 6.7 %fusion.1 = bf16[1,512,5888]{2,1,0:T(8,128)(2,1)} fusion(bf16[512,256]{1,0:T(8,128)(2,1)S(1)} %convolution_convert_fusion, bf16[512,5888]{1,0:T(8,128)(2,1)} %copy-done, f32[2944,256]{1,0:T(8,128)S(1)} %convert_add_fusion.1, f32[2944,256]{1,0:T(8,128)S(1)} %copy-done.2), kind=kOutput, calls=%fused_computation.4 | convolution fusion | flops 1561591808 | bytes 18350080 | tf_op jit(solution)/shard_map/dot_general | solution.py:138
  292.3 122.3 %all-to-all-done.1 = bf16[16,32,5888]{2,1,0:T(8,128)(2,1)} async-done(((bf16[16,32,5888]{2,1,0:T(8,128)(2,1)}), bf16[16,32,5888]{2,1,0:T(8,128)(2,1)}, u32[]{:S(2)}, u32[]{:S(2)}) %all-to-all-start.1) | async-done | bytes 6029344 | tf_op jit(solution)/shard_map/all_to_all | solution.py:128
  414.6 5.7 %copy.9 = bf16[16,32,5888]{2,1,0:T(8,128)(2,1)} copy(bf16[16,32,5888]{2,1,0:T(8,128)(2,1)} %all-to-all-done.1) | data formatting | bytes 12058624
  (11 shorter events, 0.1 us)
Async XLA Ops:
  0.6 6.7 %copy-start.4 = (bf16[1,2944,256]{2,1,0:T(8,128)(2,1)S(1)}, bf16[1,2944,256]{2,1,0:T(8,128)(2,1)}, u32[]{:S(2)}) copy-start(bf16[1,2944,256]{2,1,0:T(8,128)(2,1)} %param.6) | copy-start | bytes 4521988
  0.6 138.5 %all-to-all-start = ((bf16[16,32,5888]{2,1,0:T(8,128)(2,1)}), bf16[16,32,5888]{2,1,0:T(8,128)(2,1)}, u32[]{:S(2)}, u32[]{:S(2)}) async-start(bf16[16,32,5888]{2,1,0:T(8,128)(2,1)} %param.4), calls=%async_computation | async-start | bytes 12058624 | tf_op jit(solution)/shard_map/all_to_all | solution.py:93
  7.3 34.3 %collective-permute-start = (bf16[2944,256]{1,0:T(8,128)(2,1)S(1)}, bf16[2944,256]{1,0:T(8,128)(2,1)S(1)}, u32[]{:S(2)}, u32[]{:S(2)}) collective-permute-start(bf16[2944,256]{1,0:T(8,128)(2,1)S(1)} %bitcast.26), channel_id=1, source_target_pairs={{0,16},{16,0},{1,17},{17,1},{2,18},{18,2},{3,19},{19,3},{4,20},{20... | collective-permute-start | bytes 4521992 | tf_op jit(solution)/shard_map/ppermute | solution.py:82
  145.3 5.8 %copy-start = (bf16[512,5888]{1,0:T(8,128)(2,1)}, bf16[512,5888]{1,0:T(8,128)(2,1)S(1)}, u32[]{:S(2)}) copy-start(bf16[512,5888]{1,0:T(8,128)(2,1)S(1)} %fusion) | copy-start | bytes 18087940
  152.2 7.8 %collective-permute-start.1 = (f32[256,256]{1,0:T(8,128)S(1)}, f32[256,256]{1,0:T(8,128)S(1)}, u32[]{:S(2)}, u32[]{:S(2)}) collective-permute-start(f32[256,256]{1,0:T(8,128)S(1)} %fusion.14), channel_id=1, source_target_pairs={{0,16},{16,0},{1,17},{17,1},{2,18},{18,2},{3,19},{19,3},{4,20},{20... | collective-permute-start | bytes 786440 | tf_op jit(solution)/shard_map/ppermute | solution.py:82
  160.0 13.8 %copy-start.5 = (f32[256,256]{1,0:T(8,128)}, f32[256,256]{1,0:T(8,128)S(1)}, u32[]{:S(2)}) copy-start(f32[256,256]{1,0:T(8,128)S(1)} %add.41.gram) | copy-start | bytes 786436
  198.9 6.0 %slice-start = ((s8[6029312]{0:T(1024)(128)(4,1)}), s8[4194304]{0:T(1024)(128)(4,1)S(1)}, s32[]{:S(2)}) async-start(s8[6029312]{0:T(1024)(128)(4,1)} %bitcast.23), calls=%async_computation.2 | async-start | bytes 8388608
  200.6 4.3 %slice-start.1 = ((s8[6029312]{0:T(1024)(128)(4,1)}), s8[1835008]{0:T(1024)(128)(4,1)S(1)}, s32[]{:S(2)}) async-start(s8[6029312]{0:T(1024)(128)(4,1)} %bitcast.23), calls=%async_computation.3 | async-start | bytes 3670016
  203.6 33.6 %collective-permute-start.3 = (bf16[2944,256]{1,0:T(8,128)(2,1)S(1)}, bf16[2944,256]{1,0:T(8,128)(2,1)S(1)}, u32[]{:S(2)}, u32[]{:S(2)}) collective-permute-start(bf16[2944,256]{1,0:T(8,128)(2,1)S(1)} %get-tuple-element.10), channel_id=1, source_target_pairs={{0,16},{16,0},{1,17},{17,1},{2,18},{18,2},{3,19},{19,3},{4,20},{20... | collective-permute-start | bytes 4521992 | tf_op jit(solution)/shard_map/ppermute | solution.py:82
  205.9 63.7 %collective-permute-start.2 = (bf16[2944,256]{1,0:T(8,128)(2,1)S(1)}, bf16[2944,256]{1,0:T(8,128)(2,1)S(1)}, u32[]{:S(2)}, u32[]{:S(2)}) collective-permute-start(bf16[2944,256]{1,0:T(8,128)(2,1)S(1)} %get-tuple-element.12), channel_id=1, source_target_pairs={{0,16},{16,0},{1,17},{17,1},{2,18},{18,2},{3,19},{19,3},{4,20},{20... | collective-permute-start | bytes 4521992 | tf_op jit(solution)/shard_map/ppermute | solution.py:82
  269.9 1.6 copy-start.1
  272.0 4.4 %copy-start.3 = (bf16[5888,256]{1,0:T(8,128)(2,1)}, bf16[5888,256]{1,0:T(8,128)(2,1)S(1)}, u32[]{:S(2)}) copy-start(bf16[5888,256]{1,0:T(8,128)(2,1)S(1)} %multiply_convert_fusion.1) | copy-start | bytes 9043972
  276.4 138.3 %all-to-all-start.1 = ((bf16[16,32,5888]{2,1,0:T(8,128)(2,1)}), bf16[16,32,5888]{2,1,0:T(8,128)(2,1)}, u32[]{:S(2)}, u32[]{:S(2)}) async-start(bf16[16,32,5888]{2,1,0:T(8,128)(2,1)} %bitcast.25), calls=%async_computation.1 | async-start | bytes 12058624 | tf_op jit(solution)/shard_map/all_to_all | solution.py:128
  282.8 2.8 copy-start.2
where the time goes:
time: 421 us; the launch traced here: 420 us
  waiting for transfers between devices  318 us (76%)
  other arithmetic  36.6 us (9%)
  matrix products  23.6 us (6%)
  starting transfers between devices  17.3 us (4%)
  local copies, waits for them, and re-layouts  13.6 us (3%)
  Pallas kernels  10.4 us (2%)
    all_to_all x1, waiting for transfers between devices, body(): lax.all_to_all(update.reshape(experts, rows // experts, width), 'expert',...  122 us
    ppermute x4, waiting for transfers between devices, others(): lax.ppermute(sent, 'dp', [(i, (i + step) % dp) for i in range(dp)])  99.6 us
    all_to_all x1, waiting for transfers between devices, body(): lax.all_to_all(gradients, 'expert', split_axis=0, concat_axis=0, tiled=True)  96.2 us
    another operation x3, other arithmetic, cholesky_inverse(): lower = lax.linalg.cholesky(rest, symmetrize_input=False)  13.4 us
    another operation x3, other arithmetic, cholesky_inverse(): lower = lax.linalg.cholesky(gram[:half, :half], symmetrize_input=False)  12.5 us
  transfers between devices with their start and end apart: 6, of which 6 were waited for; matrix products, arithmetic and copies ran while one was open for 4% of the time, Pallas kernels for 0%

commit v1 on v0

v1 whole, which is shorter than its diff:
```python
import functools
import math

import jax
import jax.numpy as jnp
from jax import lax
from jax.experimental import pallas as pl
from jax.experimental.pallas import tpu as pltpu
from jax.sharding import PartitionSpec as P

decay_rate = 0.95
epsilon = 1e-06
PIECES = 4
LANES = 128
SIDE = 8
MESH = pl.DeviceIdType.MESH


def exact_dot(a, b, contract):
    return lax.dot_general(
        a,
        b,
        (((contract[0],), (contract[1],)), ((), ())),
        precision=lax.Precision.HIGHEST,
        preferred_element_type=jnp.float32,
    )


def dot(a, b, contract=(1, 0)):
    return lax.dot_general(
        a, b, (((contract[0],), (contract[1],)), ((), ())), preferred_element_type=jnp.float32
    )


def factor_inverse(work, rank):
    block = min(LANES, rank)
    wide = 2 * rank // LANES
    sub = lax.broadcasted_iota(jnp.int32, (SIDE, LANES), 0)
    lane = lax.broadcasted_iota(jnp.int32, (SIDE, block), 1)
    place = lax.broadcasted_iota(jnp.int32, (block, 2 * rank), 0)
    for start in range(0, rank, block):

        def panel(step, _, start=start):
            first = pl.multiple_of(step * SIDE, SIDE)
            rows = work[pl.ds(start + first, SIDE), :]
            square = rows[:, start : start + block]
            columns = [
                jnp.broadcast_to(
                    jnp.sum(jnp.where(lane == first + j, square, 0.0), axis=1, keepdims=True),
                    (SIDE, LANES),
                )
                for j in range(SIDE)
            ]
            subs = jnp.concatenate([sub] * wide, axis=1)
            for j in range(SIDE):
                root = lax.rsqrt(jnp.broadcast_to(columns[j][j : j + 1, :], (SIDE, LANES)))
                column = columns[j] * root
                pivot = jnp.broadcast_to(rows[j : j + 1, :], rows.shape)
                pivot = pivot * jnp.concatenate([root] * wide, axis=1)
                below = rows - jnp.concatenate([column] * wide, axis=1) * pivot
                rows = jnp.where(subs == j, pivot, jnp.where(subs > j, below, rows))
                for k in range(j + 1, SIDE):
                    columns[k] = columns[k] - column * jnp.broadcast_to(
                        column[k : k + 1, :], (SIDE, LANES)
                    )
            work[pl.ds(start + first, SIDE), :] = rows
            change = exact_dot(rows[:, start : start + block], rows, (0, 0))
            old = work[start : start + block, :]
            work[start : start + block, :] = jnp.where(place >= first + SIDE, old - change, old)
            return 0

        lax.fori_loop(0, block // SIDE, panel, 0)
        if start + block < rank:
            done = work[start : start + block, :]
            work[start + block :, :] = work[start + block :, :] - exact_dot(
                done[:, start + block : rank], done, (0, 0)
            )


def cuts(depth):
    tiles = depth // LANES
    pieces = min(PIECES, tiles)
    edges = [-(-tiles * k // pieces) * LANES for k in range(pieces + 1)]
    return list(zip(edges[:-1], edges[1:]))


def step_kernel(
    dp,
    experts,
    layers,
    gradients,
    momentum,
    right_factor,
    kept_out,
    factor_out,
    update_out,
    blended,
    held,
    factor,
    other,
    left,
    work,
    ortho,
    right,
    rounded,
    normal,
    rows_in,
    update,
    turned,
    sums,
    grad_send,
    grad_recv,
    half_send,
    half_recv,
    left_send,
    left_recv,
    pair_send,
    pair_recv,
    sum_send,
    sum_recv,
    round_send,
    round_recv,
    rows_send,
    rows_recv,
    normal_send,
    normal_recv,
    update_send,
    update_recv,
    local_sem,
):
    x = lax.axis_index("dp")
    e = lax.axis_index("expert")
    group = experts // layers
    z, s = e // group, lax.rem(e, group)
    few = gradients.shape[1]
    rows, width = momentum.shape
    depth, rank = right_factor.shape
    team = dp * group
    mine = x * group + s
    pieces = cuts(depth)

    def remote(src, dst, send, recv, to_x, to_e):
        return pltpu.make_async_remote_copy(
            src_ref=src,
            dst_ref=dst,
            send_sem=send,
            recv_sem=recv,
            device_id=(to_x, to_e),
            device_id_type=MESH,
        )

    def mate(k):
        return lax.rem(x + k, dp)

    def away(t):
        apart = (t + 1) // 2
        to = jnp.where(lax.rem(t, 2) == 1, z + apart, z - apart)
        return to, (to >= 0) & (to < layers)

    barrier = pltpu.get_barrier_semaphore()

    def greet_expert(k, _):
        pl.semaphore_signal(
            barrier, inc=1, device_id=(x, lax.rem(e + k, experts)), device_id_type=MESH
        )
        return 0

    lax.fori_loop(1, experts, greet_expert, 0)
    for k in range(1, dp):
        for m in range(group):
            pl.semaphore_signal(
                barrier, inc=1, device_id=(mate(k), z * group + m), device_id_type=MESH
            )
    local_momentum = pltpu.make_async_copy(momentum, held, local_sem.at[0])
    local_momentum.start()
    local_factor = pltpu.make_async_copy(right_factor, factor.at[x], local_sem.at[1])
    local_factor.start()
    local_grad = pltpu.make_async_copy(gradients.at[e], blended.at[e], local_sem.at[2])
    local_grad.start()
    pl.semaphore_wait(barrier, experts - 1 + (dp - 1) * group)

    factor_copies = [
        remote(right_factor, factor.at[x], pair_send.at[k - 1], pair_recv.at[k - 1], mate(k), e)
        for k in range(1, dp)
    ]
    for copy in factor_copies:
        copy.start()

    def grad_copy(to):
        return remote(
            gradients.at[to], blended.at[e], grad_send.at[to], grad_recv.at[e], x, to
        )

    def send_layer(t, _):
        to, real = away(2 * (layers - 1) - t)

        @pl.when(real)
        def _():
            def one(k, _):
                m = lax.rem(s + k, group)

                @pl.when(to * group + m != e)
                def _():
                    grad_copy(to * group + m).start()

                return 0

            lax.fori_loop(0, group, one, 0)

        return 0

    lax.fori_loop(0, 2 * layers - 1, send_layer, 0)
    local_momentum.wait()
    local_factor.wait()
    local_grad.wait()
    for copy in factor_copies:
        copy.wait_recv()

    def half_copy(k, block):
        to = mate(k)
        return remote(
            blended.at[block, :, pl.ds(pl.multiple_of(to * depth, LANES), depth)],
            other.at[k - 1, block],
            half_send.at[k - 1, block],
            half_recv.at[k - 1, block],
            to,
            e,
        )

    def left_copy(k, block):
        part = left.at[x, pl.ds(pl.multiple_of(block * few, few), few)]
        return remote(
            part, part, left_send.at[k - 1, block], left_recv.at[k - 1, block], mate(k), e
        )

    def take_layer(t, _):
        source, real = away(t)

        @pl.when(real)
        def _():
            def one(k, _):
                block = source * group + lax.rem(s + group - k, group)

                @pl.when(block != e)
                def _():
                    remote(
                        gradients.at[block], blended.at[block],
                        grad_send.at[block], grad_recv.at[block], x, block,
                    ).wait_recv()

                span = pl.ds(pl.multiple_of(block * few, few), few)
                new = (
                    decay_rate * held[span].astype(jnp.float32)
                    + blended[block].astype(jnp.float32)
                ).astype(jnp.bfloat16)
                blended[block] = new
                left[x, span] = dot(new, factor[...].reshape(dp * depth, rank))
                for k in range(1, dp):
                    half_copy(k, block).start()
                    left_copy(k, block).start()
                return 0

            lax.fori_loop(0, group, one, 0)

        return 0

    lax.fori_loop(0, 2 * layers - 1, take_layer, 0)

    def arrived(block, _):
        for k in range(1, dp):
            half_copy(k, block).wait_recv()
            left_copy(k, block).wait_recv()
        return 0

    lax.fori_loop(0, experts, arrived, 0)

    every = left[...].reshape(dp * rows, rank)
    row = lax.broadcasted_iota(jnp.int32, (rank, rank), 0)
    col = lax.broadcasted_iota(jnp.int32, (rank, rank), 1)
    work[:, :rank] = exact_dot(every, every, (0, 0))
    work[:, rank:] = jnp.where(row == col, 1.0, 0.0)
    factor_inverse(work, rank)
    inverse = work[:, rank:]
    for k in range(dp):
        ortho[k] = exact_dot(left[k], inverse, (1, 1)).astype(jnp.bfloat16)
    per = group * few

    def rows_copy(source, to):
        return remote(
            ortho.at[:, pl.ds(pl.multiple_of(to * per, per), per)],
            rows_in.at[source],
            rows_send.at[to],
            rows_recv.at[source],
            x,
            to * group + s,
        )

    def send_rows(t, _):
        to, real = away(t)

        @pl.when(real)
        def _():
            rows_copy(z, to).start()

        return 0

    own = jnp.transpose(exact_dot(left[x], inverse, (1, 1))).astype(jnp.bfloat16)
    others = [
        jnp.transpose(exact_dot(left[mate(k)], inverse, (1, 1))).astype(jnp.bfloat16)
        for k in range(1, dp)
    ]
    square = jnp.zeros((SIDE, rank), jnp.float32)
    for lo, hi in pieces:
        begin = pl.multiple_of(x * depth + lo, LANES)
        part = dot(own, blended[:, :, pl.ds(begin, hi - lo)].reshape(rows, hi - lo))
        for k in range(1, dp):
            part = part + dot(others[k - 1], other[k - 1, :, :, lo:hi].reshape(rows, hi - lo))
        right[:, lo:hi] = part
        rounded[x, :, lo:hi] = part.astype(jnp.bfloat16)
        square = square + exact_dot(
            jnp.ones((SIDE, hi - lo), jnp.float32), part * part, (1, 1)
        )
    sums[0] = square
    lax.fori_loop(1, 2 * layers - 1, send_rows, 0)
    sum_copies = [
        remote(sums.at[0], sums.at[k], sum_send.at[k - 1], sum_recv.at[k - 1], mate(k), e)
        for k in range(1, dp)
    ]
    for copy in sum_copies:
        copy.start()
    round_copies = [
        remote(rounded.at[x], rounded.at[x], round_send.at[k - 1], round_recv.at[k - 1], mate(k), e)
        for k in range(1, dp)
    ]
    for copy in round_copies:
        copy.start()
    total = square
    for k in range(1, dp):
        sum_copies[k - 1].wait_recv()
        total = total + sums[k]
    scale = lax.rsqrt(total[0:1, :] / width + epsilon)
    scale = jnp.transpose(jnp.broadcast_to(scale, (LANES, rank)))[:, 0:1]

    def normal_copy(layer, piece, side):
        lo, hi = pieces[piece]
        part = normal.at[layer, :, lo:hi]
        to = jnp.clip(z + side, 0, layers - 1)
        return remote(
            part,
            part,
            normal_send.at[layer, piece, (side + 1) // 2],
            normal_recv.at[layer, piece],
            x,
            to * group + s,
        )

    def update_copy(layer, piece, k):
        lo, hi = pieces[piece]
        to = lax.rem(mine + k, team)
        to_x, to_s = to // group, lax.rem(to, group)
        return (
            update.at[layer, to_x, pl.ds(pl.multiple_of(to_s * few, few), few), lo:hi],
            update_out.at[
                layer * group + s, :, pl.ds(pl.multiple_of(x * depth + lo, LANES), hi - lo)
            ],
            to_x,
            z * group + to_s,
        )

    def multiply(layer, piece):
        lo, hi = pieces[piece]
        result = math.sqrt(rows * dp / rank) * dot(
            rows_in[layer].reshape(dp * per, rank), normal[layer, :, lo:hi]
        )
        update[layer, :, :, lo:hi] = result.astype(jnp.bfloat16).reshape(dp, per, hi - lo)

    def scatter(layer, piece):
        src, dst, _, _ = update_copy(layer, piece, 0)
        pltpu.make_async_copy(src, dst, update_recv.at[layer, mine]).start()

        def one(k, _):
            src, dst, to_x, to_e = update_copy(layer, piece, k)
            remote(
                src, dst, update_send.at[layer, k - 1], update_recv.at[layer, mine], to_x, to_e
            ).start()
            return 0

        lax.fori_loop(1, team, one, 0)

    for piece, (lo, hi) in enumerate(pieces):
        normal[z, :, lo:hi] = (right[:, lo:hi] * scale).astype(jnp.bfloat16)
    rows_in[z] = ortho[:, pl.ds(pl.multiple_of(z * per, per), per)]
    for piece in range(len(pieces)):
        multiply(z, piece)
        for side in (1, -1):

            @pl.when((z + side >= 0) & (z + side < layers))
            def _(piece=piece, side=side):
                normal_copy(z, piece, side).start()

    for piece in range(len(pieces)):
        scatter(z, piece)

    turned[...] = jnp.transpose(normal[z].astype(jnp.float32)).astype(jnp.bfloat16)
    factor_store = pltpu.make_async_copy(turned, factor_out, local_sem.at[1])
    factor_store.start()
    for copy in round_copies:
        copy.wait_recv()
    own_rows = ortho[x]
    for k in range(dp):
        for lo, hi in pieces:
            at = slice(k * depth + lo, k * depth + hi)
            old = blended[:, :, at].reshape(rows, hi - lo).astype(jnp.float32)
            held[:, at] = (
                old - (1.0 - decay_rate) * dot(own_rows, rounded[k, :, lo:hi])
            ).astype(jnp.bfloat16)
    kept_store = pltpu.make_async_copy(held, kept_out, local_sem.at[0])
    kept_store.start()

    def far(apart, _):
        for side in (1, -1):
            layer = z - side * apart

            @pl.when((layer >= 0) & (layer < layers))
            def _():
                rows_copy(layer, z).wait_recv()

        for piece in range(len(pieces)):
            for side in (1, -1):
                layer = z - side * apart

                @pl.when((layer >= 0) & (layer < layers))
                def _(piece=piece, side=side, layer=layer):
                    normal_copy(layer, piece, side).wait_recv()

                    @pl.when((z + side >= 0) & (z + side < layers))
                    def _():
                        normal_copy(layer, piece, side).start()

                    multiply(layer, piece)
                    scatter(layer, piece)

        return 0

    lax.fori_loop(1, layers, far, 0)

    def done_block(block, _):
        @pl.when(block != e)
        def _():
            grad_copy(block).wait_send()

        for k in range(1, dp):
            half_copy(k, block).wait_send()
            left_copy(k, block).wait_send()
        return 0

    lax.fori_loop(0, experts, done_block, 0)
    for copy in factor_copies + sum_copies + round_copies:
        copy.wait_send()

    def done_layer(layer, _):
        @pl.when(layer != z)
        def _():
            rows_copy(z, layer).wait_send()

        for piece in range(len(pieces)):
            for side in (1, -1):

                @pl.when((side * (z - layer) >= 0) & (z + side >= 0) & (z + side < layers))
                def _(piece=piece, side=side):
                    normal_copy(layer, piece, side).wait_send()

        def one(k, _):
            src = update.at[layer, 0, pl.ds(0, few)]
            dst = update_out.at[layer * group, :, pl.ds(0, depth)]
            remote(
                src, dst, update_send.at[layer, k - 1], update_recv.at[layer, mine], mate(1), e
            ).wait_send()
            return 0

        lax.fori_loop(1, team, one, 0)

        def come(m, _):
            src = update.at[layer, 0, pl.ds(0, few)]
            dst = update_out.at[layer * group, :, pl.ds(0, depth)]
            pltpu.make_async_copy(src, dst, update_recv.at[layer, m]).wait()
            return 0

        lax.fori_loop(0, team, come, 0)
        return 0

    lax.fori_loop(0, layers, done_layer, 0)
    factor_store.wait()
    kept_store.wait()


def make_body(dp):
    def body(gradients, momentum, right_factor):
        experts, few, width = gradients.shape
        rows = momentum.shape[1]
        depth, rank = right_factor.shape[1:]
        group = max(1, min(experts, rank // (dp * few)))
        while experts % group:
            group -= 1
        layers = experts // group
        team = dp * group
        pieces = len(cuts(depth))
        any_space = pl.BlockSpec(memory_space=pl.ANY)
        bf16, f32 = jnp.bfloat16, jnp.float32
        dma = pltpu.SemaphoreType.DMA
        kept, own_factor, returned = pl.pallas_call(
            functools.partial(step_kernel, dp, experts, layers),
            out_shape=(
                jax.ShapeDtypeStruct((rows, width), bf16),
                jax.ShapeDtypeStruct((depth, rank), bf16),
                jax.ShapeDtypeStruct((experts, few, width), bf16),
            ),
            in_specs=[any_space] * 3,
            out_specs=(any_space,) * 3,
            scratch_shapes=[
                pltpu.VMEM((experts, few, width), bf16),
                pltpu.VMEM((rows, width), bf16),
                pltpu.VMEM((dp, depth, rank), bf16),
                pltpu.VMEM((dp - 1, experts, few, depth), bf16),
                pltpu.VMEM((dp, rows, rank), f32),
                pltpu.VMEM((rank, 2 * rank), f32),
                pltpu.VMEM((dp, rows, rank), bf16),
                pltpu.VMEM((rank, depth), f32),
                pltpu.VMEM((dp, rank, depth), bf16),
                pltpu.VMEM((layers, rank, depth), bf16),
                pltpu.VMEM((layers, dp, group * few, rank), bf16),
                pltpu.VMEM((layers, dp, group * few, depth), bf16),
                pltpu.VMEM((depth, rank), bf16),
                pltpu.VMEM((dp, SIDE, rank), f32),
                dma((experts,)),
                dma((experts,)),
                dma((dp - 1, experts)),
                dma((dp - 1, experts)),
                dma((dp - 1, experts)),
                dma((dp - 1, experts)),
                dma((dp - 1,)),
                dma((dp - 1,)),
                dma((dp - 1,)),
                dma((dp - 1,)),
                dma((dp - 1,)),
                dma((dp - 1,)),
                dma((layers,)),
                dma((layers,)),
                dma((layers, pieces, 2)),
                dma((layers, pieces)),
                dma((layers, team - 1)),
                dma((layers, team)),
                dma((3,)),
            ],
            compiler_params=pltpu.CompilerParams(
                collective_id=0, has_side_effects=True, vmem_limit_bytes=66000000
            ),
            name="dion_step",
        )(gradients, momentum[0], right_factor[0])
        return kept[None], own_factor[None], returned

    return body


def solution(mesh):
    in_specs = (P(None, ("dp", "expert"), None), P("expert", "dp", None), P("expert", "dp", None))
    out_specs = (P("expert", "dp", None), P("expert", "dp", None), P(None, ("dp", "expert"), None))
    return jax.shard_map(
        make_body(mesh.shape["dp"]),
        mesh=mesh,
        in_specs=in_specs,
        out_specs=out_specs,
        check_vma=False,
    )
```

time: 421 us -> 331 us (0.79)
  the two profiles are of different devices: /device:TPU:13 before, /device:TPU:1 now
where the time goes in v1:
time: 331 us
  Pallas kernels  320 us (97%)
  local copies, waits for them, and re-layouts  9.86 us (3%)
    pallas_call x1, Pallas kernels, body(): pl.pallas_call(functools.partial(step_kernel, dp, experts, layers), out_s...  320 us
    unnamed x9, local copies, waits for them, and re-layouts  9.86 us

profile of v1, /device:TPU:1, one launch (start us, length us, event | category | flops | bytes accessed | tf_op | source)
XLA Modules:
  0.0 330.9 jit_solution(761663225760308027)
XLA Ops:
  0.6 320.3 %dion_step.1 = (bf16[512,5888]{1,0:T(8,128)(2,1)}, bf16[2944,256]{1,0:T(8,128)(2,1)}, bf16[16,32,5888]{2,1,0:T(8,128)(2,1)}) custom-call(bf16[16,32,5888]{2,1,0:T(8,128)(2,1)} %gradients.1, bf16[512,5888]{1,0:T(8,128)(2,1)} %bitcast.4, bf16[2944,256]{1,0:T(8,128)(2,1)} %bitcast.8), custom_call_target="tpu_custom_call" | custom-call | tf_op jit(solution)/shard_map/dion_step/pallas_call | solution.py:511
  321.0 0.0 slice-start
  321.0 0.0 copy-start
  321.0 0.0 slice-start.1
  321.0 6.1 %copy.9 = bf16[1,512,5888]{2,1,0:T(8,128)(2,1)} copy(bf16[1,512,5888]{2,1,0:T(8,128)(2,1)} %bitcast.7) | data formatting | bytes 12058624
  327.1 0.0 copy-done
  327.1 1.1 copy.10
  328.2 0.0 slice-done
  328.3 0.0 slice-done.1
  328.3 2.6 copy.11
  (1 shorter events, 0.0 us)
Async XLA Ops:
  321.0 7.3 %slice-start = ((s8[6029312]{0:T(1024)(128)(4,1)}), s8[4194304]{0:T(1024)(128)(4,1)S(1)}, s32[]{:S(2)}) async-start(s8[6029312]{0:T(1024)(128)(4,1)} %bitcast.5), calls=%async_computation | async-start | bytes 8388608
  321.0 6.1 %copy-start = (bf16[2944,256]{1,0:T(8,128)(2,1)S(1)}, bf16[2944,256]{1,0:T(8,128)(2,1)}, u32[]{:S(2)}) copy-start(bf16[2944,256]{1,0:T(8,128)(2,1)} %get-tuple-element.7) | copy-start | bytes 4521988
  321.0 7.2 %slice-start.1 = ((s8[6029312]{0:T(1024)(128)(4,1)}), s8[1835008]{0:T(1024)(128)(4,1)S(1)}, s32[]{:S(2)}) async-start(s8[6029312]{0:T(1024)(128)(4,1)} %bitcast.5), calls=%async_computation.1 | async-start | bytes 3670016

commit v2 on v1

--- a/solution.py
+++ b/solution.py
@@ -11,8 +11,10 @@
 decay_rate = 0.95
 epsilon = 1e-06
 PIECES = 4
+AHEAD = 1
 LANES = 128
-SIDE = 8
+SIDE = 32
+SUBLANES = 8
 MESH = pl.DeviceIdType.MESH
 
 
@@ -34,16 +36,18 @@
 
 def factor_inverse(work, rank):
     block = min(LANES, rank)
-    wide = 2 * rank // LANES
     sub = lax.broadcasted_iota(jnp.int32, (SIDE, LANES), 0)
     lane = lax.broadcasted_iota(jnp.int32, (SIDE, block), 1)
-    place = lax.broadcasted_iota(jnp.int32, (block, 2 * rank), 0)
     for start in range(0, rank, block):
-
-        def panel(step, _, start=start):
+        end = start + block
+        low, high = start, rank + end
+        tiles = (high - low) // LANES
+        place = lax.broadcasted_iota(jnp.int32, (block, high - low), 0)
+
+        def panel(step, _, start=start, end=end, low=low, high=high, tiles=tiles, place=place):
             first = pl.multiple_of(step * SIDE, SIDE)
-            rows = work[pl.ds(start + first, SIDE), :]
-            square = rows[:, start : start + block]
+            rows = work[pl.ds(start + first, SIDE), low:high]
+            square = rows[:, :block]
             columns = [
                 jnp.broadcast_to(
                     jnp.sum(jnp.where(lane == first + j, square, 0.0), axis=1, keepdims=True),
@@ -51,29 +55,32 @@
                 )
                 for j in range(SIDE)
             ]
-            subs = jnp.concatenate([sub] * wide, axis=1)
+            parts = [rows[:, LANES * t : LANES * (t + 1)] for t in range(tiles)]
+            roots = jnp.zeros((SIDE, LANES), jnp.float32)
             for j in range(SIDE):
                 root = lax.rsqrt(jnp.broadcast_to(columns[j][j : j + 1, :], (SIDE, LANES)))
-                column = columns[j] * root
-                pivot = jnp.broadcast_to(rows[j : j + 1, :], rows.shape)
-                pivot = pivot * jnp.concatenate([root] * wide, axis=1)
-                below = rows - jnp.concatenate([column] * wide, axis=1) * pivot
-                rows = jnp.where(subs == j, pivot, jnp.where(subs > j, below, rows))
+                roots = jnp.where(sub == j, root, roots)
+                column = jnp.where(sub > j, columns[j] * root, 0.0)
                 for k in range(j + 1, SIDE):
                     columns[k] = columns[k] - column * jnp.broadcast_to(
                         column[k : k + 1, :], (SIDE, LANES)
                     )
-            work[pl.ds(start + first, SIDE), :] = rows
-            change = exact_dot(rows[:, start : start + block], rows, (0, 0))
-            old = work[start : start + block, :]
-            work[start : start + block, :] = jnp.where(place >= first + SIDE, old - change, old)
+                column = column * root
+                for t in range(tiles):
+                    pivot = jnp.broadcast_to(parts[t][j : j + 1, :], (SIDE, LANES))
+                    parts[t] = parts[t] - column * pivot
+            rows = jnp.concatenate([part * roots for part in parts], axis=1)
+            work[pl.ds(start + first, SIDE), low:high] = rows
+            change = exact_dot(rows[:, :block], rows, (0, 0))
+            old = work[start:end, low:high]
+            work[start:end, low:high] = jnp.where(place >= first + SIDE, old - change, old)
             return 0
 
         lax.fori_loop(0, block // SIDE, panel, 0)
-        if start + block < rank:
-            done = work[start : start + block, :]
-            work[start + block :, :] = work[start + block :, :] - exact_dot(
-                done[:, start + block : rank], done, (0, 0)
+        if end < rank:
+            done = work[start:end, low:high]
+            work[end:, low:high] = work[end:, low:high] - exact_dot(
+                done[:, block : rank - low], done, (0, 0)
             )
 
 
@@ -103,6 +110,7 @@
     ortho,
     right,
     rounded,
+    pair,
     normal,
     rows_in,
     update,
@@ -192,7 +200,10 @@
         )
 
     def send_layer(t, _):
-        to, real = away(2 * (layers - 1) - t)
+        near, real = away(jnp.maximum(t - 2, 0))
+        end = (near == 0) | (near == layers - 1)
+        to = jnp.where(t < 2, t * (layers - 1), near)
+        real = jnp.where(t < 2, to != z, real & ((near == z) | ~end))
 
         @pl.when(real)
         def _():
@@ -209,7 +220,7 @@
 
         return 0
 
-    lax.fori_loop(0, 2 * layers - 1, send_layer, 0)
+    lax.fori_loop(0, 2 * layers + 1, send_layer, 0)
     local_momentum.wait()
     local_factor.wait()
     local_grad.wait()
@@ -234,7 +245,12 @@
         )
 
     def take_layer(t, _):
-        source, real = away(t)
+        inner, real = away(jnp.clip(2 * layers + 1 - t, 0, 2 * layers - 2))
+        real = real & (inner != z) & (inner > 0) & (inner < layers - 1)
+        near = jnp.where(2 * z < layers, 0, layers - 1)
+        end = jnp.where(t == 1, near, layers - 1 - near)
+        source = jnp.where(t == 0, z, jnp.where(t < 3, end, inner))
+        real = jnp.where(t == 0, True, jnp.where(t < 3, end != z, real))
 
         @pl.when(real)
         def _():
@@ -264,7 +280,7 @@
 
         return 0
 
-    lax.fori_loop(0, 2 * layers - 1, take_layer, 0)
+    lax.fori_loop(0, 2 * layers + 1, take_layer, 0)
 
     def arrived(block, _):
         for k in range(1, dp):
@@ -309,17 +325,20 @@
         jnp.transpose(exact_dot(left[mate(k)], inverse, (1, 1))).astype(jnp.bfloat16)
         for k in range(1, dp)
     ]
-    square = jnp.zeros((SIDE, rank), jnp.float32)
+    square = jnp.zeros((rank, LANES), jnp.float32)
     for lo, hi in pieces:
         begin = pl.multiple_of(x * depth + lo, LANES)
         part = dot(own, blended[:, :, pl.ds(begin, hi - lo)].reshape(rows, hi - lo))
         for k in range(1, dp):
             part = part + dot(others[k - 1], other[k - 1, :, :, lo:hi].reshape(rows, hi - lo))
         right[:, lo:hi] = part
-        rounded[x, :, lo:hi] = part.astype(jnp.bfloat16)
-        square = square + exact_dot(
-            jnp.ones((SIDE, hi - lo), jnp.float32), part * part, (1, 1)
-        )
+        rounded[:, lo:hi] = part.astype(jnp.bfloat16)
+        for at in range(0, hi - lo, LANES):
+            tile = part[:, at : at + LANES]
+            square = square + tile * tile
+    square = jnp.broadcast_to(
+        jnp.sum(jnp.transpose(square), axis=0, keepdims=True), (SUBLANES, rank)
+    )
     sums[0] = square
     lax.fori_loop(1, 2 * layers - 1, send_rows, 0)
     sum_copies = [
@@ -328,12 +347,6 @@
     ]
     for copy in sum_copies:
         copy.start()
-    round_copies = [
-        remote(rounded.at[x], rounded.at[x], round_send.at[k - 1], round_recv.at[k - 1], mate(k), e)
-        for k in range(1, dp)
-    ]
-    for copy in round_copies:
-        copy.start()
     total = square
     for k in range(1, dp):
         sum_copies[k - 1].wait_recv()
@@ -341,108 +354,182 @@
     scale = lax.rsqrt(total[0:1, :] / width + epsilon)
     scale = jnp.transpose(jnp.broadcast_to(scale, (LANES, rank)))[:, 0:1]
 
-    def normal_copy(layer, piece, side):
+    def normal_copy(layer, piece, to, way):
         lo, hi = pieces[piece]
         part = normal.at[layer, :, lo:hi]
-        to = jnp.clip(z + side, 0, layers - 1)
         return remote(
             part,
             part,
-            normal_send.at[layer, piece, (side + 1) // 2],
+            normal_send.at[layer, piece, way],
             normal_recv.at[layer, piece],
             x,
             to * group + s,
         )
 
-    def update_copy(layer, piece, k):
-        lo, hi = pieces[piece]
-        to = lax.rem(mine + k, team)
-        to_x, to_s = to // group, lax.rem(to, group)
-        return (
-            update.at[layer, to_x, pl.ds(pl.multiple_of(to_s * few, few), few), lo:hi],
-            update_out.at[
-                layer * group + s, :, pl.ds(pl.multiple_of(x * depth + lo, LANES), hi - lo)
-            ],
-            to_x,
-            z * group + to_s,
-        )
+    is_end = (z == 0) | (z == layers - 1)
+    beyond = layers - 1 - z
+
+    def inside(layer):
+        return (layer >= 0) & (layer < layers)
 
     def multiply(layer, piece):
         lo, hi = pieces[piece]
-        result = math.sqrt(rows * dp / rank) * dot(
-            rows_in[layer].reshape(dp * per, rank), normal[layer, :, lo:hi]
-        )
+        result = gain * dot(rows_in[layer].reshape(dp * per, rank), normal[layer, :, lo:hi])
         update[layer, :, :, lo:hi] = result.astype(jnp.bfloat16).reshape(dp, per, hi - lo)
 
-    def scatter(layer, piece):
-        src, dst, _, _ = update_copy(layer, piece, 0)
-        pltpu.make_async_copy(src, dst, update_recv.at[layer, mine]).start()
+    def multiply_own(half, piece, source):
+        lo, hi = pieces[piece]
+        begin = pl.multiple_of(half * depth + lo, LANES)
+        result = gain * dot(ortho[x, pl.ds(pl.multiple_of(z * per, per), per)], source[:, lo:hi])
+        update[z, half, :, lo:hi] = result.astype(jnp.bfloat16)
+
+        def place(to_s):
+            return (
+                update.at[z, half, pl.ds(pl.multiple_of(to_s * few, few), few), lo:hi],
+                update_out.at[e, :, pl.ds(begin, hi - lo)],
+            )
+
+        src, dst = place(s)
+        pltpu.make_async_copy(src, dst, update_recv.at[z, mine]).start()
 
         def one(k, _):
-            src, dst, to_x, to_e = update_copy(layer, piece, k)
+            to_s = lax.rem(s + k, group)
+            src, dst = place(to_s)
             remote(
-                src, dst, update_send.at[layer, k - 1], update_recv.at[layer, mine], to_x, to_e
+                src, dst, update_send.at[z, k - 1], update_recv.at[z, mine], x, z * group + to_s
             ).start()
             return 0
 
+        lax.fori_loop(1, group, one, 0)
+
+    def scatter(layer, piece):
+        lo, hi = pieces[piece]
+        begin = pl.multiple_of(x * depth + lo, LANES)
+
+        def place(to_x, to_s):
+            return (
+                update.at[layer, to_x, pl.ds(pl.multiple_of(to_s * few, few), few), lo:hi],
+                update_out.at[layer * group + s, :, pl.ds(begin, hi - lo)],
+            )
+
+        src, dst = place(x, s)
+        pltpu.make_async_copy(src, dst, update_recv.at[layer, mine]).start()
+
+        def one(k, _):
+            to = lax.rem(mine + k, team)
+            to_x, to_s = to // group, lax.rem(to, group)
+            src, dst = place(to_x, to_s)
+            remote(
+                src,
+                dst,
+                update_send.at[layer, k - 1],
+                update_recv.at[layer, mine],
+                to_x,
+                z * group + to_s,
+            ).start()
+            return 0
+
         lax.fori_loop(1, team, one, 0)
 
+    gain = math.sqrt(rows * dp / rank)
     for piece, (lo, hi) in enumerate(pieces):
         normal[z, :, lo:hi] = (right[:, lo:hi] * scale).astype(jnp.bfloat16)
-    rows_in[z] = ortho[:, pl.ds(pl.multiple_of(z * per, per), per)]
+
+    def onward(layer, side):
+        to = z + side
+        last = ((layer == 0) & (to == layers - 1)) | ((layer == layers - 1) & (to == 0))
+        return inside(to) & (side * (z - layer) >= 0) & ~last
+
     for piece in range(len(pieces)):
-        multiply(z, piece)
+        if piece == AHEAD:
+
+            @pl.when(is_end & (z != beyond))
+            def _():
+                for whole in range(len(pieces)):
+                    normal_copy(z, whole, beyond, 2).start()
+
         for side in (1, -1):
 
-            @pl.when((z + side >= 0) & (z + side < layers))
+            @pl.when(onward(z, side))
             def _(piece=piece, side=side):
-                normal_copy(z, piece, side).start()
-
+                normal_copy(z, piece, z + side, (side + 1) // 2).start()
+
+    pair_copies = [
+        remote(normal.at[z], pair.at[k - 1], round_send.at[k - 1], round_recv.at[k - 1], mate(k), e)
+        for k in range(1, dp)
+    ]
+    for copy in pair_copies:
+        copy.start()
     for piece in range(len(pieces)):
-        scatter(z, piece)
+        multiply_own(x, piece, normal.at[z])
 
     turned[...] = jnp.transpose(normal[z].astype(jnp.float32)).astype(jnp.bfloat16)
     factor_store = pltpu.make_async_copy(turned, factor_out, local_sem.at[1])
     factor_store.start()
-    for copy in round_copies:
-        copy.wait_recv()
-    own_rows = ortho[x]
-    for k in range(dp):
+
+    def keep(half):
         for lo, hi in pieces:
-            at = slice(k * depth + lo, k * depth + hi)
+            at = pl.ds(pl.multiple_of(half * depth + lo, LANES), hi - lo)
             old = blended[:, :, at].reshape(rows, hi - lo).astype(jnp.float32)
             held[:, at] = (
-                old - (1.0 - decay_rate) * dot(own_rows, rounded[k, :, lo:hi])
+                old - (1.0 - decay_rate) * dot(ortho[x], rounded[:, lo:hi])
             ).astype(jnp.bfloat16)
+
+    keep(x)
+
+    def come(layer, piece, side):
+        normal_copy(layer, piece, z, 0).wait_recv()
+
+        @pl.when(onward(layer, side))
+        def _():
+            normal_copy(layer, piece, z + side, (side + 1) // 2).start()
+
+        multiply(layer, piece)
+        scatter(layer, piece)
+
+    @pl.when(is_end & (z != beyond))
+    def _():
+        rows_copy(beyond, z).wait_recv()
+        for piece in range(len(pieces)):
+            normal_copy(beyond, piece, z, 0).wait_recv()
+            multiply(beyond, piece)
+            scatter(beyond, piece)
+
+    def far(apart, _):
+        for side in (1, -1):
+
+            @pl.when(inside(z - side * apart))
+            def _(side=side):
+                rows_copy(z - side * apart, z).wait_recv()
+
+        for piece in range(len(pieces)):
+            for side in (1, -1):
+
+                @pl.when(inside(z - side * apart))
+                def _(piece=piece, side=side):
+                    come(z - side * apart, piece, side)
+
+        @pl.when(apart == 1)
+        def _():
+            partners()
+
+        return 0
+
+    def partners():
+        for k in range(1, dp):
+            pair_copies[k - 1].wait_recv()
+            for piece, (lo, hi) in enumerate(pieces):
+                multiply_own(mate(k), piece, pair.at[k - 1])
+                rounded[:, lo:hi] = (
+                    pair[k - 1, :, lo:hi].astype(jnp.float32) / scale
+                ).astype(jnp.bfloat16)
+            keep(mate(k))
+
+    if layers < 3:
+        partners()
+    lax.fori_loop(1, layers - 1, far, 0)
     kept_store = pltpu.make_async_copy(held, kept_out, local_sem.at[0])
     kept_store.start()
-
-    def far(apart, _):
-        for side in (1, -1):
-            layer = z - side * apart
-
-            @pl.when((layer >= 0) & (layer < layers))
-            def _():
-                rows_copy(layer, z).wait_recv()
-
-        for piece in range(len(pieces)):
-            for side in (1, -1):
-                layer = z - side * apart
-
-                @pl.when((layer >= 0) & (layer < layers))
-                def _(piece=piece, side=side, layer=layer):
-                    normal_copy(layer, piece, side).wait_recv()
-
-                    @pl.when((z + side >= 0) & (z + side < layers))
-                    def _():
-                        normal_copy(layer, piece, side).start()
-
-                    multiply(layer, piece)
-                    scatter(layer, piece)
-
-        return 0
-
-    lax.fori_loop(1, layers, far, 0)
 
     def done_block(block, _):
         @pl.when(block != e)
@@ -455,7 +542,7 @@
         return 0
 
     lax.fori_loop(0, experts, done_block, 0)
-    for copy in factor_copies + sum_copies + round_copies:
+    for copy in factor_copies + sum_copies + pair_copies:
         copy.wait_send()
 
     def done_layer(layer, _):
@@ -465,28 +552,52 @@
 
         for piece in range(len(pieces)):
             for side in (1, -1):
-
-                @pl.when((side * (z - layer) >= 0) & (z + side >= 0) & (z + side < layers))
+                @pl.when(onward(layer, side))
                 def _(piece=piece, side=side):
-                    normal_copy(layer, piece, side).wait_send()
-
-        def one(k, _):
+                    normal_copy(layer, piece, z, (side + 1) // 2).wait_send()
+
+            @pl.when((layer == beyond) & (layer != z) & is_end)
+            def _(piece=piece):
+                normal_copy(z, piece, layer, 2).wait_send()
+
+        @pl.when(layer == z)
+        def _():
+            def gone(k, _):
+                remote(
+                    gradients.at[0], update_out.at[e],
+                    update_send.at[z, k - 1], update_recv.at[z, mine], mate(1), e,
+                ).wait_send()
+                return 0
+
+            lax.fori_loop(1, group, gone, 0)
+
+            def came(m, _):
+                pltpu.make_async_copy(
+                    gradients.at[0], update_out.at[e], update_recv.at[z, x * group + m]
+                ).wait()
+                return 0
+
+            lax.fori_loop(0, group, came, 0)
+
+        @pl.when(layer != z)
+        def _():
             src = update.at[layer, 0, pl.ds(0, few)]
             dst = update_out.at[layer * group, :, pl.ds(0, depth)]
-            remote(
-                src, dst, update_send.at[layer, k - 1], update_recv.at[layer, mine], mate(1), e
-            ).wait_send()
-            return 0
-
-        lax.fori_loop(1, team, one, 0)
-
-        def come(m, _):
-            src = update.at[layer, 0, pl.ds(0, few)]
-            dst = update_out.at[layer * group, :, pl.ds(0, depth)]
-            pltpu.make_async_copy(src, dst, update_recv.at[layer, m]).wait()
-            return 0
-
-        lax.fori_loop(0, team, come, 0)
+
+            def gone(k, _):
+                remote(
+                    src, dst, update_send.at[layer, k - 1], update_recv.at[layer, mine], mate(1), e
+                ).wait_send()
+                return 0
+
+            lax.fori_loop(1, team, gone, 0)
+
+            def came(m, _):
+                pltpu.make_async_copy(src, dst, update_recv.at[layer, m]).wait()
+                return 0
+
+            lax.fori_loop(0, team, came, 0)
+
         return 0
 
     lax.fori_loop(0, layers, done_layer, 0)
@@ -526,12 +637,13 @@
                 pltpu.VMEM((rank, 2 * rank), f32),
                 pltpu.VMEM((dp, rows, rank), bf16),
                 pltpu.VMEM((rank, depth), f32),
-                pltpu.VMEM((dp, rank, depth), bf16),
+                pltpu.VMEM((rank, depth), bf16),
+                pltpu.VMEM((dp - 1, rank, depth), bf16),
                 pltpu.VMEM((layers, rank, depth), bf16),
                 pltpu.VMEM((layers, dp, group * few, rank), bf16),
                 pltpu.VMEM((layers, dp, group * few, depth), bf16),
                 pltpu.VMEM((depth, rank), bf16),
-                pltpu.VMEM((dp, SIDE, rank), f32),
+                pltpu.VMEM((dp, SUBLANES, rank), f32),
                 dma((experts,)),
                 dma((experts,)),
                 dma((dp - 1, experts)),
@@ -546,7 +658,7 @@
                 dma((dp - 1,)),
                 dma((layers,)),
                 dma((layers,)),
-                dma((layers, pieces, 2)),
+                dma((layers, pieces, 3)),
                 dma((layers, pieces)),
                 dma((layers, team - 1)),
                 dma((layers, team)),

time: 331 us -> 270 us (0.82)
  Pallas kernels: 320 us -> 260 us
    pallas_call x1, Pallas kernels: 320 us -> 260 us  [body(): pl.pallas_call(functools.partial(step_kernel, dp, experts, layers), out_s...]
where the time goes in v2:
time: 270 us
  Pallas kernels  260 us (96%)
  local copies, waits for them, and re-layouts  9.86 us (4%)
    pallas_call x1, Pallas kernels, body(): pl.pallas_call(functools.partial(step_kernel, dp, experts, layers), out_s...  260 us
    unnamed x9, local copies, waits for them, and re-layouts  9.86 us

profile of v2, /device:TPU:1, one launch (start us, length us, event | category | flops | bytes accessed | tf_op | source)
XLA Modules:
  0.0 270.2 jit_solution(7986988717672405250)
XLA Ops:
  0.6 259.7 %dion_step.1 = (bf16[512,5888]{1,0:T(8,128)(2,1)}, bf16[2944,256]{1,0:T(8,128)(2,1)}, bf16[16,32,5888]{2,1,0:T(8,128)(2,1)}) custom-call(bf16[16,32,5888]{2,1,0:T(8,128)(2,1)} %gradients.1, bf16[512,5888]{1,0:T(8,128)(2,1)} %bitcast.4, bf16[2944,256]{1,0:T(8,128)(2,1)} %bitcast.8), custom_call_target="tpu_custom_call" | custom-call | tf_op jit(solution)/shard_map/dion_step/pallas_call | solution.py:622
  260.3 0.0 slice-start
  260.3 0.0 copy-start
  260.3 0.0 slice-start.1
  260.3 6.1 %copy.9 = bf16[1,512,5888]{2,1,0:T(8,128)(2,1)} copy(bf16[1,512,5888]{2,1,0:T(8,128)(2,1)} %bitcast.7) | data formatting | bytes 12058624
  266.4 0.0 copy-done
  266.4 1.1 copy.10
  267.6 0.0 slice-done
  267.6 0.0 slice-done.1
  267.6 2.6 copy.11
  (1 shorter events, 0.0 us)
Async XLA Ops:
  260.3 7.3 %slice-start = ((s8[6029312]{0:T(1024)(128)(4,1)}), s8[4194304]{0:T(1024)(128)(4,1)S(1)}, s32[]{:S(2)}) async-start(s8[6029312]{0:T(1024)(128)(4,1)} %bitcast.5), calls=%async_computation | async-start | bytes 8388608
  260.3 6.1 %copy-start = (bf16[2944,256]{1,0:T(8,128)(2,1)S(1)}, bf16[2944,256]{1,0:T(8,128)(2,1)}, u32[]{:S(2)}) copy-start(bf16[2944,256]{1,0:T(8,128)(2,1)} %get-tuple-element.7) | copy-start | bytes 4521988
  260.3 7.2 %slice-start.1 = ((s8[6029312]{0:T(1024)(128)(4,1)}), s8[1835008]{0:T(1024)(128)(4,1)S(1)}, s32[]{:S(2)}) async-start(s8[6029312]{0:T(1024)(128)(4,1)} %bitcast.5), calls=%async_computation.1 | async-start | bytes 3670016

commit v3 on v2

--- a/solution.py
+++ b/solution.py
@@ -11,7 +11,6 @@
 decay_rate = 0.95
 epsilon = 1e-06
 PIECES = 4
-AHEAD = 1
 LANES = 128
 SIDE = 32
 SUBLANES = 8
@@ -98,11 +97,10 @@
     gradients,
     momentum,
     right_factor,
-    kept_out,
-    factor_out,
+    held,
+    turned,
     update_out,
     blended,
-    held,
     factor,
     other,
     left,
@@ -114,7 +112,6 @@
     normal,
     rows_in,
     update,
-    turned,
     sums,
     grad_send,
     grad_recv,
@@ -160,6 +157,8 @@
     def mate(k):
         return lax.rem(x + k, dp)
 
+    near_end = jnp.where(2 * z < layers, 0, layers - 1)
+
     def away(t):
         apart = (t + 1) // 2
         to = jnp.where(lax.rem(t, 2) == 1, z + apart, z - apart)
@@ -200,10 +199,12 @@
         )
 
     def send_layer(t, _):
-        near, real = away(jnp.maximum(t - 2, 0))
-        end = (near == 0) | (near == layers - 1)
-        to = jnp.where(t < 2, t * (layers - 1), near)
-        real = jnp.where(t < 2, to != z, real & ((near == z) | ~end))
+        last = t > 2 * layers - 2
+        inner, real = away(jnp.minimum(t, 2 * layers - 2))
+        real = real & ((inner == z) | ((inner > 0) & (inner < layers - 1)))
+        end = jnp.where(t == 2 * layers - 1, near_end, layers - 1 - near_end)
+        to = jnp.where(last, end, inner)
+        real = jnp.where(last, end != z, real)
 
         @pl.when(real)
         def _():
@@ -245,12 +246,8 @@
         )
 
     def take_layer(t, _):
-        inner, real = away(jnp.clip(2 * layers + 1 - t, 0, 2 * layers - 2))
-        real = real & (inner != z) & (inner > 0) & (inner < layers - 1)
-        near = jnp.where(2 * z < layers, 0, layers - 1)
-        end = jnp.where(t == 1, near, layers - 1 - near)
-        source = jnp.where(t == 0, z, jnp.where(t < 3, end, inner))
-        real = jnp.where(t == 0, True, jnp.where(t < 3, end != z, real))
+        at_end = (z == 0) | (z == layers - 1)
+        source, real = away(jnp.where(at_end & (t > 2), 2 * layers + 1 - t, t))
 
         @pl.when(real)
         def _():
@@ -272,23 +269,22 @@
                 blended[block] = new
                 left[x, span] = dot(new, factor[...].reshape(dp * depth, rank))
                 for k in range(1, dp):
+                    left_copy(k, block).start()
                     half_copy(k, block).start()
-                    left_copy(k, block).start()
                 return 0
 
             lax.fori_loop(0, group, one, 0)
 
         return 0
 
-    lax.fori_loop(0, 2 * layers + 1, take_layer, 0)
-
-    def arrived(block, _):
+    lax.fori_loop(0, 2 * layers - 1, take_layer, 0)
+
+    def left_arrived(block, _):
         for k in range(1, dp):
-            half_copy(k, block).wait_recv()
             left_copy(k, block).wait_recv()
         return 0
 
-    lax.fori_loop(0, experts, arrived, 0)
+    lax.fori_loop(0, experts, left_arrived, 0)
 
     every = left[...].reshape(dp * rows, rank)
     row = lax.broadcasted_iota(jnp.int32, (rank, rank), 0)
@@ -325,6 +321,13 @@
         jnp.transpose(exact_dot(left[mate(k)], inverse, (1, 1))).astype(jnp.bfloat16)
         for k in range(1, dp)
     ]
+
+    def half_arrived(block, _):
+        for k in range(1, dp):
+            half_copy(k, block).wait_recv()
+        return 0
+
+    lax.fori_loop(0, experts, half_arrived, 0)
     square = jnp.zeros((rank, LANES), jnp.float32)
     for lo, hi in pieces:
         begin = pl.multiple_of(x * depth + lo, LANES)
@@ -340,13 +343,13 @@
         jnp.sum(jnp.transpose(square), axis=0, keepdims=True), (SUBLANES, rank)
     )
     sums[0] = square
-    lax.fori_loop(1, 2 * layers - 1, send_rows, 0)
     sum_copies = [
         remote(sums.at[0], sums.at[k], sum_send.at[k - 1], sum_recv.at[k - 1], mate(k), e)
         for k in range(1, dp)
     ]
     for copy in sum_copies:
         copy.start()
+    lax.fori_loop(1, 2 * layers - 1, send_rows, 0)
     total = square
     for k in range(1, dp):
         sum_copies[k - 1].wait_recv()
@@ -365,9 +368,6 @@
             x,
             to * group + s,
         )
-
-    is_end = (z == 0) | (z == layers - 1)
-    beyond = layers - 1 - z
 
     def inside(layer):
         return (layer >= 0) & (layer < layers)
@@ -436,18 +436,9 @@
         normal[z, :, lo:hi] = (right[:, lo:hi] * scale).astype(jnp.bfloat16)
 
     def onward(layer, side):
-        to = z + side
-        last = ((layer == 0) & (to == layers - 1)) | ((layer == layers - 1) & (to == 0))
-        return inside(to) & (side * (z - layer) >= 0) & ~last
+        return inside(z + side) & (side * (z - layer) >= 0)
 
     for piece in range(len(pieces)):
-        if piece == AHEAD:
-
-            @pl.when(is_end & (z != beyond))
-            def _():
-                for whole in range(len(pieces)):
-                    normal_copy(z, whole, beyond, 2).start()
-
         for side in (1, -1):
 
             @pl.when(onward(z, side))
@@ -464,8 +455,6 @@
         multiply_own(x, piece, normal.at[z])
 
     turned[...] = jnp.transpose(normal[z].astype(jnp.float32)).astype(jnp.bfloat16)
-    factor_store = pltpu.make_async_copy(turned, factor_out, local_sem.at[1])
-    factor_store.start()
 
     def keep(half):
         for lo, hi in pieces:
@@ -477,43 +466,29 @@
 
     keep(x)
 
-    def come(layer, piece, side):
+    def come(layer, piece):
         normal_copy(layer, piece, z, 0).wait_recv()
-
-        @pl.when(onward(layer, side))
-        def _():
-            normal_copy(layer, piece, z + side, (side + 1) // 2).start()
+        for side in (1, -1):
+
+            @pl.when(onward(layer, side))
+            def _(side=side):
+                normal_copy(layer, piece, z + side, (side + 1) // 2).start()
 
         multiply(layer, piece)
         scatter(layer, piece)
 
-    @pl.when(is_end & (z != beyond))
-    def _():
-        rows_copy(beyond, z).wait_recv()
-        for piece in range(len(pieces)):
-            normal_copy(beyond, piece, z, 0).wait_recv()
-            multiply(beyond, piece)
-            scatter(beyond, piece)
-
-    def far(apart, _):
-        for side in (1, -1):
-
-            @pl.when(inside(z - side * apart))
-            def _(side=side):
-                rows_copy(z - side * apart, z).wait_recv()
-
-        for piece in range(len(pieces)):
-            for side in (1, -1):
-
-                @pl.when(inside(z - side * apart))
-                def _(piece=piece, side=side):
-                    come(z - side * apart, piece, side)
-
-        @pl.when(apart == 1)
-        def _():
-            partners()
-
-        return 0
+    def inner(t, _):
+        layer, real = away(t)
+
+        @pl.when(real & (layer > 0) & (layer < layers - 1))
+        def _():
+            rows_copy(layer, z).wait_recv()
+            for piece in range(len(pieces)):
+                come(layer, piece)
+
+        return 0
+
+    lax.fori_loop(1, 2 * layers - 1, inner, 0)
 
     def partners():
         for k in range(1, dp):
@@ -525,11 +500,19 @@
                 ).astype(jnp.bfloat16)
             keep(mate(k))
 
-    if layers < 3:
-        partners()
-    lax.fori_loop(1, layers - 1, far, 0)
-    kept_store = pltpu.make_async_copy(held, kept_out, local_sem.at[0])
-    kept_store.start()
+    partners()
+    def end_layer(t, _):
+        layer = jnp.where(t == 0, near_end, layers - 1 - near_end)
+
+        @pl.when((layer != z) & ((t == 0) | (layers > 1)))
+        def _():
+            rows_copy(layer, z).wait_recv()
+            for piece in range(len(pieces)):
+                come(layer, piece)
+
+        return 0
+
+    lax.fori_loop(0, 2, end_layer, 0)
 
     def done_block(block, _):
         @pl.when(block != e)
@@ -555,10 +538,6 @@
                 @pl.when(onward(layer, side))
                 def _(piece=piece, side=side):
                     normal_copy(layer, piece, z, (side + 1) // 2).wait_send()
-
-            @pl.when((layer == beyond) & (layer != z) & is_end)
-            def _(piece=piece):
-                normal_copy(z, piece, layer, 2).wait_send()
 
         @pl.when(layer == z)
         def _():
@@ -601,8 +580,6 @@
         return 0
 
     lax.fori_loop(0, layers, done_layer, 0)
-    factor_store.wait()
-    kept_store.wait()
 
 
 def make_body(dp):
@@ -622,15 +599,14 @@
         kept, own_factor, returned = pl.pallas_call(
             functools.partial(step_kernel, dp, experts, layers),
             out_shape=(
-                jax.ShapeDtypeStruct((rows, width), bf16),
-                jax.ShapeDtypeStruct((depth, rank), bf16),
-                jax.ShapeDtypeStruct((experts, few, width), bf16),
+                pltpu.VMEM((rows, width), bf16),
+                pltpu.VMEM((depth, rank), bf16),
+                pltpu.VMEM((experts, few, width), bf16),
             ),
             in_specs=[any_space] * 3,
-            out_specs=(any_space,) * 3,
+            out_specs=(pl.BlockSpec(memory_space=pltpu.VMEM),) * 3,
             scratch_shapes=[
                 pltpu.VMEM((experts, few, width), bf16),
-                pltpu.VMEM((rows, width), bf16),
                 pltpu.VMEM((dp, depth, rank), bf16),
                 pltpu.VMEM((dp - 1, experts, few, depth), bf16),
                 pltpu.VMEM((dp, rows, rank), f32),
@@ -642,7 +618,6 @@
                 pltpu.VMEM((layers, rank, depth), bf16),
                 pltpu.VMEM((layers, dp, group * few, rank), bf16),
                 pltpu.VMEM((layers, dp, group * few, depth), bf16),
-                pltpu.VMEM((depth, rank), bf16),
                 pltpu.VMEM((dp, SUBLANES, rank), f32),
                 dma((experts,)),
                 dma((experts,)),
@@ -658,14 +633,14 @@
                 dma((dp - 1,)),
                 dma((layers,)),
                 dma((layers,)),
-                dma((layers, pieces, 3)),
+                dma((layers, pieces, 2)),
                 dma((layers, pieces)),
                 dma((layers, team - 1)),
                 dma((layers, team)),
                 dma((3,)),
             ],
             compiler_params=pltpu.CompilerParams(
-                collective_id=0, has_side_effects=True, vmem_limit_bytes=66000000
+                collective_id=0, has_side_effects=True, vmem_limit_bytes=46000000
             ),
             name="dion_step",
         )(gradients, momentum[0], right_factor[0])

time: 270 us -> 262 us (0.970)
  Pallas kernels: 260 us -> 253 us
  local copies, waits for them, and re-layouts: 9.86 us -> 6.36 us
    pallas_call x1, Pallas kernels: 260 us -> 253 us  [body(): pl.pallas_call(functools.partial(step_kernel, dp, experts, layers), out_s...]
    unnamed x9 -> x3, local copies, waits for them, and re-layouts: 9.86 us -> 6.36 us
where the time goes in v3:
time: 262 us; the launch traced here: 260 us
  Pallas kernels  253 us (97%)
  local copies, waits for them, and re-layouts  6.36 us (2%)
    pallas_call x1, Pallas kernels, body(): pl.pallas_call(functools.partial(step_kernel, dp, experts, layers), out_s...  253 us
    unnamed x3, local copies, waits for them, and re-layouts  6.36 us

profile of v3, /device:TPU:1, one launch (start us, length us, event | category | flops | bytes accessed | tf_op | source)
XLA Modules:
  0.0 260.4 jit_solution(3384015060542391038)
XLA Ops:
  0.6 253.4 %dion_step.1 = (bf16[512,5888]{1,0:T(8,128)(2,1)S(1)}, bf16[2944,256]{1,0:T(8,128)(2,1)S(1)}, bf16[16,32,5888]{2,1,0:T(8,128)(2,1)S(1)}) custom-call(bf16[16,32,5888]{2,1,0:T(8,128)(2,1)} %gradients.1, bf16[512,5888]{1,0:T(8,128)(2,1)} %bitcast.6, bf16[2944,256]{1,0:T(8,128)(2,1)} %bitcast.7), custom_call_target="tpu_custom_call" | custom-call | tf_op jit(solution)/shard_map/dion_step/pallas_call | solution.py:599
  254.0 2.6 %copy.9 = bf16[1,512,5888]{2,1,0:T(8,128)(2,1)} copy(bf16[1,512,5888]{2,1,0:T(8,128)(2,1)S(1)} %bitcast.4) | data formatting | bytes 12058624
  256.6 1.1 copy.10
  257.8 2.6 %copy.11 = bf16[16,32,5888]{2,1,0:T(8,128)(2,1)} copy(bf16[16,32,5888]{2,1,0:T(8,128)(2,1)S(1)} %get-tuple-element.11) | data formatting | bytes 12058624

commit v4 on v3

--- a/solution.py
+++ b/solution.py
@@ -127,6 +127,8 @@
     round_recv,
     rows_send,
     rows_recv,
+    share_send,
+    share_recv,
     normal_send,
     normal_recv,
     update_send,
@@ -299,12 +301,18 @@
 
     def rows_copy(source, to):
         return remote(
-            ortho.at[:, pl.ds(pl.multiple_of(to * per, per), per)],
-            rows_in.at[source],
+            ortho.at[x, pl.ds(pl.multiple_of(to * per, per), per)],
+            rows_in.at[source, x],
             rows_send.at[to],
             rows_recv.at[source],
             x,
             to * group + s,
+        )
+
+    def share_copy(source, k):
+        part = rows_in.at[source, x]
+        return remote(
+            part, part, share_send.at[k - 1, source], share_recv.at[k - 1, source], mate(k), e
         )
 
     def send_rows(t, _):
@@ -445,6 +453,16 @@
             def _(piece=piece, side=side):
                 normal_copy(z, piece, z + side, (side + 1) // 2).start()
 
+    def share(layer, wanted):
+        @pl.when(wanted & (layer != z))
+        def _():
+            rows_copy(layer, z).wait_recv()
+            for k in range(1, dp):
+                share_copy(layer, k).start()
+
+        return 0
+
+    lax.fori_loop(1, layers - 1, lambda layer, _: share(layer, z >= 0), 0)
     pair_copies = [
         remote(normal.at[z], pair.at[k - 1], round_send.at[k - 1], round_recv.at[k - 1], mate(k), e)
         for k in range(1, dp)
@@ -474,6 +492,9 @@
             def _(side=side):
                 normal_copy(layer, piece, z + side, (side + 1) // 2).start()
 
+        if piece == 0:
+            for k in range(1, dp):
+                share_copy(layer, k).wait_recv()
         multiply(layer, piece)
         scatter(layer, piece)
 
@@ -482,10 +503,11 @@
 
         @pl.when(real & (layer > 0) & (layer < layers - 1))
         def _():
-            rows_copy(layer, z).wait_recv()
             for piece in range(len(pieces)):
                 come(layer, piece)
 
+        for end in sorted({0, layers - 1}):
+            share(end, t == 2)
         return 0
 
     lax.fori_loop(1, 2 * layers - 1, inner, 0)
@@ -506,7 +528,6 @@
 
         @pl.when((layer != z) & ((t == 0) | (layers > 1)))
         def _():
-            rows_copy(layer, z).wait_recv()
             for piece in range(len(pieces)):
                 come(layer, piece)
 
@@ -532,6 +553,8 @@
         @pl.when(layer != z)
         def _():
             rows_copy(z, layer).wait_send()
+            for k in range(1, dp):
+                share_copy(layer, k).wait_send()
 
         for piece in range(len(pieces)):
             for side in (1, -1):
@@ -633,6 +656,8 @@
                 dma((dp - 1,)),
                 dma((layers,)),
                 dma((layers,)),
+                dma((dp - 1, layers)),
+                dma((dp - 1, layers)),
                 dma((layers, pieces, 2)),
                 dma((layers, pieces)),
                 dma((layers, team - 1)),

time: 262 us -> 258 us (0.985)
  no operation moved by 1% of the time
where the time goes in v4:
time: 258 us
  Pallas kernels  251 us (97%)
  local copies, waits for them, and re-layouts  6.36 us (2%)
    pallas_call x1, Pallas kernels, body(): pl.pallas_call(functools.partial(step_kernel, dp, experts, layers), out_s...  251 us
    unnamed x3, local copies, waits for them, and re-layouts  6.36 us

profile of v4, /device:TPU:1, one launch (start us, length us, event | category | flops | bytes accessed | tf_op | source)
XLA Modules:
  0.0 257.9 jit_solution(5975655133952268146)
XLA Ops:
  0.6 250.9 %dion_step.1 = (bf16[512,5888]{1,0:T(8,128)(2,1)S(1)}, bf16[2944,256]{1,0:T(8,128)(2,1)S(1)}, bf16[16,32,5888]{2,1,0:T(8,128)(2,1)S(1)}) custom-call(bf16[16,32,5888]{2,1,0:T(8,128)(2,1)} %gradients.1, bf16[512,5888]{1,0:T(8,128)(2,1)} %bitcast.6, bf16[2944,256]{1,0:T(8,128)(2,1)} %bitcast.7), custom_call_target="tpu_custom_call" | custom-call | tf_op jit(solution)/shard_map/dion_step/pallas_call | solution.py:622
  251.5 2.6 %copy.9 = bf16[1,512,5888]{2,1,0:T(8,128)(2,1)} copy(bf16[1,512,5888]{2,1,0:T(8,128)(2,1)S(1)} %bitcast.4) | data formatting | bytes 12058624
  254.2 1.1 copy.10
  255.3 2.6 %copy.11 = bf16[16,32,5888]{2,1,0:T(8,128)(2,1)} copy(bf16[16,32,5888]{2,1,0:T(8,128)(2,1)S(1)} %get-tuple-element.11) | data formatting | bytes 12058624
